TPU v7x, 32 devices: a whole 2x2x4 slice. The times are simulated.
32 devices in a mesh: pair: 8 (over z, x), aux: 4 (over y, core).
Axes of the slice: x: 2, y: 2, z: 4, core: 2. Of those that a mesh axis runs over, the one named last changes fastest.
Arguments:
- panels: bfloat16 [16, 120, 9216], P('pair', None, 'aux'), may hold values from -1.5 to 1.5
- amplitudes: bfloat16 [16, 2, 120, 120], P('pair'), may hold values from -0.5 to 0.5
- drive: float32 [16, 2, 14400], P('pair', None, 'aux'), may hold values from -6 to 6
- pno_energy: float32 [16, 120], P('pair'), may hold values from 1 to 3
- occ_energy: float32 [32], replicated, may hold values from -2 to -0.5
- frequency: float32 [1], replicated, may hold values from 0.2 to 2
- pair_lmo: int32 [16, 2], replicated, may hold values from 0 to 31
- neighbours: int32 [16, 8], P('pair'), may hold values from 0 to 15
- pno_ranks: int32 [16], P('pair'), may hold values from 60 to 120
- fock_off: float32 [32, 32], replicated, may hold values from -1.8 to 1.8
Outputs:
- residual: float32 [16, 2, 14400], P('pair', None, 'aux')
Inputs may be any that keep to these rules, and one draw needn't show every extreme that they name: `neighbours`: neighbour pairs; a pair may be listed more than once and may list itself. `pno_ranks`: rows of a pair's panel from its rank on are padding.
All inputs are finite; a program needn't handle non-finite values.
Results may differ from a plain program's by a relative error of at most 0.0033.
Values may be sent and summed in bfloat16 or wider, within the bound.
A program may use at most 128 MiB of HBM per device.

v0:
```python
import math

import jax
import jax.numpy as jnp
from jax import lax
from jax.sharding import PartitionSpec as P


def pair_weights(pair_lmo, neighbours, fock_off, first_pair):
    local_pairs = neighbours.shape[0]
    total_pairs = pair_lmo.shape[0]
    lmo_count = fock_off.shape[0]
    lmo_ids = jnp.arange(lmo_count, dtype=jnp.int32)
    own_lmo = lax.dynamic_slice_in_dim(pair_lmo, first_pair, local_pairs, 0)
    own_table = (own_lmo[:, :, None] == lmo_ids[None, None, :]).astype(jnp.float32)
    lmo_table = (pair_lmo[:, :, None] == lmo_ids[None, None, :]).astype(jnp.float32)
    pair_ids = jnp.arange(total_pairs, dtype=jnp.int32)
    onehot = (neighbours[:, :, None] == pair_ids[None, None, :]).astype(jnp.float32)
    fock_rows = jnp.einsum("psl,lm->psm", own_table, fock_off, precision=lax.Precision.HIGHEST)
    near_table = jnp.einsum("pkn,nsl->pksl", onehot, lmo_table)
    values = jnp.sum(fock_rows[:, None, :, :] * near_table, axis=(2, 3))
    weights = jnp.sum(values[:, :, None] * onehot, axis=1).astype(jnp.bfloat16)
    return (weights, own_table)


def project_pairs(slab, amp_block):
    group_size = slab.shape[0]
    matrices = jnp.transpose(amp_block, (0, 2, 1, 3)).reshape(group_size, amp_block.shape[2], -1)
    return jnp.einsum("nra,nrc->nac", slab, matrices, preferred_element_type=jnp.float32).astype(
        jnp.bfloat16
    )


def accumulate(weights, group_limit, running_sum, arriving):
    slab_rows, amp_rows = arriving
    pair_count = slab_rows.shape[0]
    group_size = math.gcd(pair_count, group_limit)

    def group_turn(turn_index, partial_sum):
        offset = turn_index * group_size
        slab = lax.dynamic_slice_in_dim(slab_rows, offset, group_size, 0)
        amp_block = lax.dynamic_slice_in_dim(amp_rows, offset, group_size, 0)
        projected = project_pairs(slab, amp_block)
        coeff_block = lax.dynamic_slice_in_dim(weights, offset, group_size, 1)
        return partial_sum + jnp.einsum(
            "pn,nac->pac", coeff_block, projected, preferred_element_type=jnp.float32
        )

    return lax.fori_loop(0, pair_count // group_size, group_turn, running_sum)


def close_coupling(masked, collected_sum, freq_count):
    local_pairs, rank_dim, aux_width = masked.shape
    collected = collected_sum.astype(jnp.bfloat16)
    coupled = jnp.einsum("pra,pac->prc", masked, collected, preferred_element_type=jnp.float32)
    coupled = jnp.transpose(
        coupled.reshape(local_pairs, rank_dim, freq_count, rank_dim), (0, 2, 1, 3)
    )
    return coupled.reshape(local_pairs, freq_count, rank_dim * rank_dim)


def body(
    panels,
    amplitudes,
    drive,
    pno_energy,
    occ_energy,
    frequency,
    pair_lmo,
    neighbours,
    pno_ranks,
    fock_off,
):
    local_pairs, rank_dim, aux_width = panels.shape
    first_pair = lax.axis_index("pair") * local_pairs
    rows_index = jnp.arange(rank_dim, dtype=jnp.int32)
    keep_rows = rows_index[None, :] < pno_ranks[:, None]
    masked = jnp.where(keep_rows[:, :, None], panels, jnp.zeros_like(panels))
    weights, own_table = pair_weights(pair_lmo, neighbours, fock_off, first_pair)
    start_sum = jnp.zeros((local_pairs, aux_width, 2 * rank_dim), jnp.float32)
    collected_sum = accumulate(
        weights,
        4,
        start_sum,
        (
            lax.all_gather(masked, "pair", axis=0, tiled=True),
            lax.all_gather(amplitudes, "pair", axis=0, tiled=True),
        ),
    )
    coupled_terms = close_coupling(masked, collected_sum, 2)
    coupled_share = lax.psum_scatter(coupled_terms, "aux", scatter_dimension=2, tiled=True)
    share_width = drive.shape[2]
    share_start = lax.axis_index("aux") * share_width
    occ_pair = jnp.sum(own_table * occ_energy[None, None, :], axis=(1, 2))
    shift = pno_energy[:, :, None] + pno_energy[:, None, :] - occ_pair[:, None, None]
    shift_flat = lax.dynamic_slice_in_dim(
        shift.reshape(local_pairs, rank_dim * rank_dim), share_start, share_width, 1
    )
    signs = jnp.array([1.0, -1.0], jnp.float32)
    factor = shift_flat[:, None, :] - signs[None, :, None] * frequency[0]
    amp_flat = amplitudes.reshape(local_pairs, 2, rank_dim * rank_dim)
    amp_share = lax.dynamic_slice_in_dim(amp_flat, share_start, share_width, 2).astype(jnp.float32)
    return drive + factor * amp_share + coupled_share


def solution(mesh):
    placed = (
        P("pair", None, "aux"),
        P("pair", None, None, None),
        P("pair", None, "aux"),
        P("pair", None),
        P(),
        P(),
        P(),
        P("pair", None),
        P("pair"),
        P(),
    )
    return jax.shard_map(
        body, mesh=mesh, in_specs=placed, out_specs=P("pair", None, "aux"), check_vma=False
    )
```

profile of v0, /device:TPU:0, one launch (start us, length us, event | category | flops | bytes accessed | tf_op | source)
XLA Modules:
  0.0 319.1 jit_solution(4289958824527709440)
XLA Ops:
  6.5 0.7 iota_compare_fusion.4
  7.3 2.4 broadcast_select_fusion
  9.8 0.8 constant_dynamic-slice_fusion.2
  10.6 0.8 broadcast_add_fusion
  11.5 0.2 add.67
  11.7 0.8 select_reduce_fusion.1
  12.5 0.2 fusion.8
  12.7 1.0 fusion.7
  13.7 0.8 select_reduce_fusion
  14.5 39.0 %all_gather.7 = bf16[16,2,120,120]{3,2,1,0:T(8,128)(2,1)S(1)} all-gather(bf16[2,2,120,120]{3,2,1,0:T(8,128)(2,1)} %param.14), channel_id=1, replica_groups=mesh['pair'=8,'aux'=4] {'pair'}, dimensions={0}, use_global_device_ids=true | all-gather | bytes 1036800 | tf_op jit(solution)/shard_map/all_gather | solution.py:87
  53.5 97.1 %all-gather.2.cloned.1.call-done = bf16[16,120,2304]{2,1,0:T(8,128)(2,1)} async-done(((bf16[2,120,2304]{2,1,0:T(8,128)(2,1)}), bf16[16,120,2304]{2,1,0:T(8,128)(2,1)}) %all-gather.2.cloned.1.call-update) | async-done | bytes 8847376 | tf_op jit(solution)/shard_map/all_gather | solution.py:86
  150.5 55.8 %while.14 = (s32[]{:T(128)}, f32[2,2304,240]{1,0,2:T(2,128)}, bf16[2,16]{1,0:T(2,128)(2,1)S(1)}, bf16[16,120,2304]{2,1,0:T(8,128)(2,1)}, bf16[16,2,120,120]{3,2,...) while((s32[]{:T(128)}, f32[2,2304,240]{1,0,2:T(2,128)}, ...), condition=%wide.region_4.5_spmd.clone, body=%wide.region_3.4_spmd.clone.sunk | while | flops 544112640 | bytes 21058792 | solution.py:49
  150.7 5.0 %convolution_convert_fusion.2 = bf16[4,2304,240]{1,2,0:T(8,128)(2,1)} fusion(bf16[4,120,240]{1,2,0:T(8,128)(2,1)S(1)} %bitcast.35, bf16[16,120,2304]{2,1,0:T(8,128)(2,1)} %get-tuple-element.185, s32[]{:T(128)S(6)} %select_n.26), kind=kOutput, calls=%fused_computation.clone.1 | convolution fusion | flops 533053440 | bytes 6865924 | tf_op jit(solution)/shard_map/while/body/eval_jaxpr/nra,nrc->nac/dot_general | solution.py:29
  155.8 7.7 %convolution_add_fusion.2 = f32[2,2304,240]{1,0,2:T(2,128)} fusion(f32[2,2304,240]{1,0,2:T(2,128)} %get-tuple-element.174, bf16[4,2304,240]{1,2,0:T(8,128)(2,1)} %convolution_convert_fusion.2, pred[]{:T(512)S(6)} %compare.3, bf16[2,16]{1,0:T(2,128)(2,1)S(1)} %get-tuple-element.184, s32[]{:T(128)S(6)} %select_n.26), kind=kOutput, calls=%fused_computation.1.clone.1 | convolution fusion | flops 11059200 | bytes 13271109 | tf_op jit(solution)/shard_map/while/body/eval_jaxpr/pn,nac->pac/dot_general | solution.py:45
  163.5 0.2 copy.39
  163.7 5.0 %convolution_convert_fusion.2 = bf16[4,2304,240]{1,2,0:T(8,128)(2,1)} fusion(bf16[4,120,240]{1,2,0:T(8,128)(2,1)S(1)} %bitcast.35, bf16[16,120,2304]{2,1,0:T(8,128)(2,1)} %get-tuple-element.185, s32[]{:T(128)S(6)} %select_n.26), kind=kOutput, calls=%fused_computation.clone.1 | convolution fusion | flops 533053440 | bytes 6865924 | tf_op jit(solution)/shard_map/while/body/eval_jaxpr/nra,nrc->nac/dot_general | solution.py:29
  168.7 9.1 %convolution_add_fusion.2 = f32[2,2304,240]{1,0,2:T(2,128)} fusion(f32[2,2304,240]{1,0,2:T(2,128)} %get-tuple-element.174, bf16[4,2304,240]{1,2,0:T(8,128)(2,1)} %convolution_convert_fusion.2, pred[]{:T(512)S(6)} %compare.3, bf16[2,16]{1,0:T(2,128)(2,1)S(1)} %get-tuple-element.184, s32[]{:T(128)S(6)} %select_n.26), kind=kOutput, calls=%fused_computation.1.clone.1 | convolution fusion | flops 11059200 | bytes 13271109 | tf_op jit(solution)/shard_map/while/body/eval_jaxpr/pn,nac->pac/dot_general | solution.py:45
  178.0 5.0 %convolution_convert_fusion.2 = bf16[4,2304,240]{1,2,0:T(8,128)(2,1)} fusion(bf16[4,120,240]{1,2,0:T(8,128)(2,1)S(1)} %bitcast.35, bf16[16,120,2304]{2,1,0:T(8,128)(2,1)} %get-tuple-element.185, s32[]{:T(128)S(6)} %select_n.26), kind=kOutput, calls=%fused_computation.clone.1 | convolution fusion | flops 533053440 | bytes 6865924 | tf_op jit(solution)/shard_map/while/body/eval_jaxpr/nra,nrc->nac/dot_general | solution.py:29
  183.0 9.1 %convolution_add_fusion.2 = f32[2,2304,240]{1,0,2:T(2,128)} fusion(f32[2,2304,240]{1,0,2:T(2,128)} %get-tuple-element.174, bf16[4,2304,240]{1,2,0:T(8,128)(2,1)} %convolution_convert_fusion.2, pred[]{:T(512)S(6)} %compare.3, bf16[2,16]{1,0:T(2,128)(2,1)S(1)} %get-tuple-element.184, s32[]{:T(128)S(6)} %select_n.26), kind=kOutput, calls=%fused_computation.1.clone.1 | convolution fusion | flops 11059200 | bytes 13271109 | tf_op jit(solution)/shard_map/while/body/eval_jaxpr/pn,nac->pac/dot_general | solution.py:45
  192.2 5.0 %convolution_convert_fusion.2 = bf16[4,2304,240]{1,2,0:T(8,128)(2,1)} fusion(bf16[4,120,240]{1,2,0:T(8,128)(2,1)S(1)} %bitcast.35, bf16[16,120,2304]{2,1,0:T(8,128)(2,1)} %get-tuple-element.185, s32[]{:T(128)S(6)} %select_n.26), kind=kOutput, calls=%fused_computation.clone.1 | convolution fusion | flops 533053440 | bytes 6865924 | tf_op jit(solution)/shard_map/while/body/eval_jaxpr/nra,nrc->nac/dot_general | solution.py:29
  197.3 9.1 %convolution_add_fusion.2 = f32[2,2304,240]{1,0,2:T(2,128)} fusion(f32[2,2304,240]{1,0,2:T(2,128)} %get-tuple-element.174, bf16[4,2304,240]{1,2,0:T(8,128)(2,1)} %convolution_convert_fusion.2, pred[]{:T(512)S(6)} %compare.3, bf16[2,16]{1,0:T(2,128)(2,1)S(1)} %get-tuple-element.184, s32[]{:T(128)S(6)} %select_n.26), kind=kOutput, calls=%fused_computation.1.clone.1 | convolution fusion | flops 11059200 | bytes 13271109 | tf_op jit(solution)/shard_map/while/body/eval_jaxpr/pn,nac->pac/dot_general | solution.py:45
  206.3 3.9 %convert_element_type.21 = bf16[2,2304,240]{1,0,2:T(2,128)(2,1)S(1)} convert(f32[2,2304,240]{1,0,2:T(2,128)} %get-tuple-element.99) | non-fusion elementwise | flops 1105920 | bytes 6635520 | tf_op jit(solution)/shard_map/convert_element_type | solution.py:54
  210.2 0.9 fusion.5
  211.1 0.2 reshape.54
  211.3 12.1 %copy.29 = f32[2,2,120,120]{1,0,3,2:T(2,128)} copy(f32[2,2,120,120]{3,1,2,0:T(2,128)S(1)} %bitcast.37) | data formatting | bytes 460800
  223.3 14.5 %reshape.61 = f32[14400,4]{1,0:T(8,128)} reshape(f32[14400,2,2]{2,1,0:T(2,128)} %bitcast.34) | data formatting | bytes 460800
  238.0 0.8 copy-done.2
  238.8 0.3 reshape.53
  239.8 62.6 %reduce-scatter.4.cloned.1.call-done = f32[3600,4]{1,0:T(8,128)} async-done(((f32[14400,4]{1,0:T(8,128)}), f32[3600,4]{1,0:T(8,128)}) %reduce-scatter.4.cloned.1.call-update) | async-done | bytes 57616
  302.5 4.9 %reshape.62 = f32[3600,2,2]{2,1,0:T(2,128)} reshape(f32[3600,4]{1,0:T(8,128)} %reduce-scatter.4.cloned.1.call-done) | data formatting | bytes 115200
  307.3 4.2 %copy.28 = f32[2,2,3600]{2,1,0:T(2,128)S(1)} copy(f32[2,2,3600]{1,0,2:T(2,128)} %bitcast.36) | data formatting | bytes 115200
  311.5 0.7 add_add_fusion
  (24 shorter events, 0.9 us)
Async XLA Ops:
  6.5 6.0 %copy-start = (f32[32,32]{1,0:T(8,128)S(1)}, f32[32,32]{1,0:T(8,128)}, u32[]{:S(2)}) copy-start(f32[32,32]{1,0:T(8,128)} %param.22) | copy-start | bytes 12292
  6.5 144.0 %all-gather.2.cloned.1.call-start = ((), (), s32[]{:S(2)}) async-start(), calls=%async_computation.1 | async-start | bytes 9953280 | tf_op jit(solution)/shard_map/all_gather | solution.py:86
  9.7 292.7 %reduce-scatter.4.cloned.1.call-start = ((), (), s32[]{:S(2)}) async-start(), calls=%async_computation.2 | async-start | bytes 9216000
  206.3 3.9 %copy-start.1 = (bf16[2,120,2304]{2,1,0:T(8,128)(2,1)S(1)}, bf16[2,120,2304]{2,1,0:T(8,128)(2,1)}, u32[]{:S(2)}) copy-start(bf16[2,120,2304]{2,1,0:T(8,128)(2,1)} %broadcast_select_fusion) | copy-start | bytes 3317764
  237.9 0.9 copy-start.2
  237.9 1.9 copy-start.4
  239.8 71.7 %copy-start.3 = (f32[2,2,3600]{2,1,0:T(2,128)S(1)}, f32[2,2,3600]{2,1,0:T(2,128)}, u32[]{:S(2)}) copy-start(f32[2,2,3600]{2,1,0:T(2,128)} %param.15) | copy-start | bytes 172804
Sparse Core Ops, SparseCore 0:
  9.8 140.6 all-gather.1
  238.0 64.3 reduce-scatter.3
where the time goes:
time: 320 us; the launch traced here: 319 us
  waiting for transfers between devices  160 us (50%)
  matrix products  57 us (18%)
  blocking collectives  39 us (12%)
  local copies, waits for them, and re-layouts  38.8 us (12%)
  between operations  14.2 us (4%)
  other arithmetic  10.3 us (3%)
    all_gather x1, waiting for transfers between devices, body(): lax.all_gather(masked, 'pair', axis=0, tiled=True)  97.1 us
    unnamed x3, waiting for transfers between devices  62.7 us
    all_gather x1, blocking collectives, body(): lax.all_gather(amplitudes, 'pair', axis=0, tiled=True)  39 us
    unnamed x14, local copies, waits for them, and re-layouts  36.5 us
    dot_general x4, matrix products, group_turn(): jnp.einsum('pn,nac->pac', coeff_block, projected, preferred_element_type=...  34.9 us
    dot_general x4, matrix products, project_pairs(): jnp.einsum('nra,nrc->nac', slab, matrices, preferred_element_type=jnp.flo...  20.1 us
  transfers between devices with their start and end apart: 2, of which 2 were waited for; matrix products, arithmetic and copies ran while one was open for 2% of the time, Pallas kernels for 0%

commit v1 on v0

v1 whole, which is shorter than its diff:
```python
import jax
import jax.numpy as jnp
from jax import lax
from jax.sharding import PartitionSpec as P


def pair_weights(pair_lmo, neighbours, fock_off, first_pair):
    local_pairs = neighbours.shape[0]
    total_pairs = pair_lmo.shape[0]
    lmo_count = fock_off.shape[0]
    lmo_ids = jnp.arange(lmo_count, dtype=jnp.int32)
    own_lmo = lax.dynamic_slice_in_dim(pair_lmo, first_pair, local_pairs, 0)
    own_table = (own_lmo[:, :, None] == lmo_ids[None, None, :]).astype(jnp.float32)
    lmo_table = (pair_lmo[:, :, None] == lmo_ids[None, None, :]).astype(jnp.float32)
    pair_ids = jnp.arange(total_pairs, dtype=jnp.int32)
    onehot = (neighbours[:, :, None] == pair_ids[None, None, :]).astype(jnp.float32)
    fock_rows = jnp.einsum("psl,lm->psm", own_table, fock_off, precision=lax.Precision.HIGHEST)
    near_table = jnp.einsum("pkn,nsl->pksl", onehot, lmo_table)
    values = jnp.sum(fock_rows[:, None, :, :] * near_table, axis=(2, 3))
    weights = jnp.sum(values[:, :, None] * onehot, axis=1).astype(jnp.bfloat16)
    return (weights, own_table)


def body(
    panels,
    amplitudes,
    drive,
    pno_energy,
    occ_energy,
    frequency,
    pair_lmo,
    neighbours,
    pno_ranks,
    fock_off,
):
    local_pairs, rank_dim, aux_width = panels.shape
    total_pairs = pair_lmo.shape[0]
    n_pair = lax.axis_size("pair")
    n_aux = lax.axis_size("aux")
    first_pair = lax.axis_index("pair") * local_pairs
    rows_index = jnp.arange(rank_dim, dtype=jnp.int32)
    keep_rows = rows_index[None, :] < pno_ranks[:, None]
    weights, own_table = pair_weights(pair_lmo, neighbours, fock_off, first_pair)
    weights = lax.all_gather(weights, "pair", axis=0, tiled=True)
    amps = jnp.where(keep_rows[:, :, None, None], jnp.transpose(amplitudes, (0, 2, 1, 3)), 0)
    amps = lax.all_gather(
        amps.reshape(local_pairs * rank_dim, 2 * rank_dim), "pair", axis=0, tiled=True
    )
    masked = jnp.where(keep_rows[:, :, None], panels, jnp.zeros_like(panels))
    slices = lax.all_to_all(
        masked.reshape(local_pairs * rank_dim, aux_width), "pair", 1, 0, tiled=True
    )
    products = jnp.einsum("iq,jq->ij", slices, slices, preferred_element_type=jnp.float32)
    products = products.reshape(total_pairs, rank_dim, total_pairs, rank_dim)
    mixed = (products * weights.astype(jnp.float32)[:, None, :, None]).astype(jnp.bfloat16)
    mixed = mixed.reshape(total_pairs * rank_dim, total_pairs * rank_dim)
    coupled = jnp.dot(mixed, amps, preferred_element_type=jnp.float32).astype(jnp.bfloat16)
    share_width = drive.shape[2]
    coupled = coupled.reshape(total_pairs, rank_dim, 2, rank_dim).transpose(0, 2, 1, 3)
    coupled = coupled.reshape(n_pair, local_pairs, 2, n_aux, share_width).transpose(0, 3, 1, 2, 4)
    coupled = coupled.reshape(n_pair * n_aux, local_pairs, 2, share_width)
    coupled = lax.all_to_all(coupled, ("pair", "aux"), 0, 0, tiled=True)
    coupled_share = jnp.sum(coupled.astype(jnp.float32), axis=0)
    share_start = lax.axis_index("aux") * share_width
    occ_pair = jnp.sum(own_table * occ_energy[None, None, :], axis=(1, 2))
    shift = pno_energy[:, :, None] + pno_energy[:, None, :] - occ_pair[:, None, None]
    shift_flat = lax.dynamic_slice_in_dim(
        shift.reshape(local_pairs, rank_dim * rank_dim), share_start, share_width, 1
    )
    signs = jnp.array([1.0, -1.0], jnp.float32)
    factor = shift_flat[:, None, :] - signs[None, :, None] * frequency[0]
    amp_flat = amplitudes.reshape(local_pairs, 2, rank_dim * rank_dim)
    amp_share = lax.dynamic_slice_in_dim(amp_flat, share_start, share_width, 2).astype(jnp.float32)
    return drive + factor * amp_share + coupled_share


def solution(mesh):
    placed = (
        P("pair", None, "aux"),
        P("pair", None, None, None),
        P("pair", None, "aux"),
        P("pair", None),
        P(),
        P(),
        P(),
        P("pair", None),
        P("pair"),
        P(),
    )
    return jax.shard_map(
        body, mesh=mesh, in_specs=placed, out_specs=P("pair", None, "aux"), check_vma=False
    )
```

time: 320 us -> 152 us (0.47)
  waiting for transfers between devices: 160 us -> 22.5 us
  matrix products: 57 us -> 11.4 us
  blocking collectives: 39 us -> 70.4 us
  between operations: 14.2 us -> 0.86 us
  starting transfers between devices: 0.04 us -> 10.9 us
  local copies, waits for them, and re-layouts: 38.8 us -> 30.6 us
  other arithmetic: 10.3 us -> 4.79 us
    all_gather x1 -> x0, waiting for transfers between devices: 97.1 us -> none  [body(): lax.all_gather(masked, 'pair', axis=0, tiled=True)]
    unnamed x3 -> x0, waiting for transfers between devices: 62.7 us -> none
    dot_general x9 -> x2, matrix products: 55.9 us -> 10.9 us  [the longest x1 5.48 us: body(): jnp.einsum('iq,jq->ij', slices, slices, preferred_element_type=jnp.float32)]
    unnamed x14 -> x24, local copies, waits for them, and re-layouts: 36.5 us -> 0.05 us
    all_gather x1 -> x2, blocking collectives: 39 us -> 70.4 us  [the longest x1 37.1 us: body(): lax.all_gather(amps.reshape(local_pairs * rank_dim, 2 * rank_dim), 'pair'...]
    all_to_all x0 -> x2, waiting for transfers between devices: none -> 22.5 us  [the longest x1 22.5 us: body(): coupled = lax.all_to_all(coupled, ('pair', 'aux'), 0, 0, tiled=True)]
    reshape x1 -> x5, local copies, waits for them, and re-layouts: 0.2 us -> 19 us  [the longest x1 14.8 us: body(): mixed = mixed.reshape(total_pairs * rank_dim, total_pairs * rank_dim)]
    all_to_all x0 -> x2, starting transfers between devices: none -> 10.9 us  [the longest x1 7.41 us: body(): lax.all_to_all(masked.reshape(local_pairs * rank_dim, aux_width), 'pair',...]
  transfers between devices with their start and end apart: 2 -> 2, of which waited for: 2 -> 1; matrix products, arithmetic and copies ran while one was open for 2% -> 2% of each run, Pallas kernels for 0% -> 0%
where the time goes in v1:
time: 152 us
  blocking collectives  70.4 us (46%)
  local copies, waits for them, and re-layouts  30.6 us (20%)
  waiting for transfers between devices  22.5 us (15%)
  matrix products  11.4 us (8%)
  starting transfers between devices  10.9 us (7%)
  other arithmetic  4.79 us (3%)
    all_gather x1, blocking collectives, body(): lax.all_gather(amps.reshape(local_pairs * rank_dim, 2 * rank_dim), 'pair'...  37.1 us
    all_gather x1, blocking collectives, body(): weights = lax.all_gather(weights, 'pair', axis=0, tiled=True)  33.4 us
    all_to_all x1, waiting for transfers between devices, body(): coupled = lax.all_to_all(coupled, ('pair', 'aux'), 0, 0, tiled=True)  22.5 us
    reshape x1, local copies, waits for them, and re-layouts, body(): mixed = mixed.reshape(total_pairs * rank_dim, total_pairs * rank_dim)  14.8 us
    all_to_all x1, starting transfers between devices, body(): lax.all_to_all(masked.reshape(local_pairs * rank_dim, aux_width), 'pair',...  7.41 us
    dot_general x1, matrix products, body(): jnp.einsum('iq,jq->ij', slices, slices, preferred_element_type=jnp.float32)  5.48 us
    dot_general x1, matrix products, body(): jnp.dot(mixed, amps, preferred_element_type=jnp.float32)  5.42 us
    convert_element_type x1, local copies, waits for them, and re-layouts, body(): (products * weights.astype(jnp.float32)[:, None, :, None]).astype(jnp.bfl...  4.73 us
  transfers between devices with their start and end apart: 2, of which 1 were waited for; matrix products, arithmetic and copies ran while one was open for 2% of the time, Pallas kernels for 0%

profile of v1, /device:TPU:0, one launch (start us, length us, event | category | flops | bytes accessed | tf_op | source)
XLA Modules:
  0.0 151.5 jit_solution(6438213021010279309)
XLA Ops:
  0.0 0.7 iota_compare_fusion.4
  0.7 1.4 broadcast_select_fusion
  2.1 1.5 copy.23
  3.6 1.6 %all_to_all.15 = bf16[240,8,288]{0,2,1:T(8,128)(2,1)} reshape(bf16[2,120,2304]{1,0,2:T(2,128)(2,1)S(1)} %copy.23) | data formatting | bytes 2211840 | tf_op jit(solution)/shard_map/all_to_all | solution.py:50
  5.2 7.4 %all-to-all-start = ((bf16[240,8,288]{0,2,1:T(8,128)(2,1)}), bf16[240,8,288]{0,2,1:T(8,128)(2,1)S(1)}, u32[]{:S(2)}, u32[]{:S(2)}) async-start(bf16[240,8,288]{0,2,1:T(8,128)(2,1)} %all_to_all.15), calls=%async_computation | async-start | bytes 2359296 | tf_op jit(solution)/shard_map/all_to_all | solution.py:50
  12.7 0.1 copy.22
  12.8 0.2 fusion.4
  13.0 0.3 fusion.3
  13.4 33.4 %all-gather = bf16[8,2,16]{2,1,0:T(2,128)(2,1)S(1)} all-gather(bf16[1,2,16]{2,1,0:T(2,128)(2,1)S(1)} %bitcast.47), channel_id=1, replica_groups=mesh['pair'=8,'aux'=4] {'pair'}, dimensions={0}, use_global_device_ids=true | all-gather | bytes 576 | tf_op jit(solution)/shard_map/all_gather | solution.py:44
  46.8 0.6 convert
  47.4 0.1 select_bitcast_fusion
  47.5 0.1 copy.28
  47.6 0.1 reshape.87
  47.7 37.1 %all_gather.7 = bf16[1920,240]{1,0:T(8,128)(2,1)} all-gather(bf16[240,240]{1,0:T(8,128)(2,1)S(1)} %reshape.87), channel_id=1, replica_groups=mesh['pair'=8,'aux'=4] {'pair'}, dimensions={0}, use_global_device_ids=true | all-gather | bytes 1036800 | tf_op jit(solution)/shard_map/all_gather | solution.py:46
  84.8 0.7 copy.24
  85.4 0.7 dot_general.14
  86.1 5.5 %multiply_convert_fusion = bf16[16,120,16,120]{3,1,2,0:T(8,128)(2,1)S(1)} fusion(f32[16,16]{1,0:T(8,128)} %convert, bf16[16,120,288,1]{1,0,2,3:T(8,128)(2,1)S(1)} %bitcast.45, bf16[16,120,288]{1,0,2:T(8,128)(2,1)S(1)} %dot_general.14), kind=kOutput, calls=%fused_computation | convolution fusion | flops 2130739200 | bytes 9585664 | tf_op jit(solution)/shard_map/iq,jq->ij/dot_general | solution.py:53
  91.6 4.7 %copy.27 = bf16[16,120,16,120]{3,2,1,0:T(8,128)(2,1)} copy(bf16[16,120,16,120]{3,1,2,0:T(8,128)(2,1)S(1)} %multiply_convert_fusion) | data formatting | bytes 14745600 | tf_op jit(solution)/shard_map/convert_element_type | solution.py:55
  96.3 14.8 %reshape.86 = bf16[1920,1920]{1,0:T(8,128)(2,1)} reshape(bf16[16,120,16,120]{3,2,1,0:T(8,128)(2,1)} %copy.27) | data formatting | bytes 14745600 | tf_op jit(solution)/shard_map/reshape | solution.py:56
  111.1 5.4 %convolution_convert_fusion = bf16[1920,240]{0,1:T(8,128)(2,1)S(1)} fusion(bf16[1920,1920]{1,0:T(8,128)(2,1)} %reshape.86, bf16[1920,240]{1,0:T(8,128)(2,1)S(1)} %copy-done.1), kind=kOutput, calls=%fused_computation.1 | convolution fusion | flops 1769932800 | bytes 9216000 | tf_op jit(solution)/shard_map/dot_general | solution.py:57
  116.5 2.0 %reshape.88 = bf16[16,120,2,120]{1,0,3,2:T(8,128)(2,1)S(1)} reshape(bf16[1920,240]{0,1:T(8,128)(2,1)S(1)} %convolution_convert_fusion) | data formatting | bytes 1843200 | tf_op jit(solution)/shard_map/reshape | solution.py:59
  118.6 0.9 copy.29
  119.4 1.2 reshape.89
  120.6 1.7 %copy.30 = bf16[8,4,2,2,3600]{4,3,2,1,0:T(2,128)(2,1)} copy(bf16[8,4,2,2,3600]{4,1,3,2,0:T(4,128)(2,1)S(1)} %bitcast.44) | data formatting | bytes 1843200 | tf_op jit(solution)/shard_map/transpose | solution.py:60
  122.4 3.5 %all-to-all-start.1 = ((bf16[32,2,2,3600]{3,2,1,0:T(2,128)(2,1)}), bf16[32,2,2,3600]{3,2,1,0:T(2,128)(2,1)S(1)}, u32[]{:S(2)}, u32[]{:S(2)}) async-start(bf16[32,2,2,3600]{3,2,1,0:T(2,128)(2,1)} %bitcast.13), calls=%async_computation.1 | async-start | bytes 1900544 | tf_op jit(solution)/shard_map/all_to_all | solution.py:62
  125.9 0.3 reshape.85
  126.4 0.2 add.33
  127.2 0.2 select_reduce_fusion.1
  127.4 0.1 dynamic-slice_subtract_fusion
  127.5 22.5 %all-to-all-done.1 = bf16[32,2,2,3600]{3,2,1,0:T(2,128)(2,1)S(1)} async-done(((bf16[32,2,2,3600]{3,2,1,0:T(2,128)(2,1)}), bf16[32,2,2,3600]{3,2,1,0:T(2,128)(2,1)S(1)}, u32[]{:S(2)}, u32[]{:S(2)}) %all-to-all-start.1) | async-done | bytes 921632 | tf_op jit(solution)/shard_map/all_to_all | solution.py:62
  150.0 0.8 convert_reduce_fusion
  150.8 0.7 add_add_fusion
  (29 shorter events, 0.3 us)
Async XLA Ops:
  0.0 12.8 %copy-start = (f32[32,32]{1,0:T(8,128)S(1)}, f32[32,32]{1,0:T(8,128)}, u32[]{:S(2)}) copy-start(f32[32,32]{1,0:T(8,128)} %param.20) | copy-start | bytes 12292
  5.2 7.4 %copy-start.8 = (s32[16,2]{0,1:T(2,128)S(1)}, s32[16,2]{0,1:T(2,128)}, u32[]{:S(2)}) copy-start(s32[16,2]{0,1:T(2,128)} %param.17) | copy-start | bytes 388
  5.2 7.8 %copy-start.9 = (s32[2,8]{1,0:T(2,128)S(1)}, s32[2,8]{1,0:T(2,128)}, u32[]{:S(2)}) copy-start(s32[2,8]{1,0:T(2,128)} %param.18) | copy-start | bytes 196
  5.2 42.2 %copy-start.2 = (bf16[2,2,120,120]{3,2,1,0:T(8,128)(2,1)S(1)}, bf16[2,2,120,120]{3,2,1,0:T(8,128)(2,1)}, u32[]{:S(2)}) copy-start(bf16[2,2,120,120]{3,2,1,0:T(8,128)(2,1)} %param.12) | copy-start | bytes 345604
  5.2 79.6 %all-to-all-start = ((bf16[240,8,288]{0,2,1:T(8,128)(2,1)}), bf16[240,8,288]{0,2,1:T(8,128)(2,1)S(1)}, u32[]{:S(2)}, u32[]{:S(2)}) async-start(bf16[240,8,288]{0,2,1:T(8,128)(2,1)} %all_to_all.15), calls=%async_computation | async-start | bytes 2359296 | tf_op jit(solution)/shard_map/all_to_all | solution.py:50
  12.8 34.7 %copy-start.6 = (s32[2,2]{1,0:T(2,128)}, s32[2,2]{1,0:T(2,128)S(1)}, u32[]{:S(2)}) copy-start(s32[2,2]{1,0:T(2,128)S(1)} %copy.22) | copy-start | bytes 52
  96.3 14.8 %copy-start.1 = (bf16[1920,240]{1,0:T(8,128)(2,1)S(1)}, bf16[1920,240]{1,0:T(8,128)(2,1)}, u32[]{:S(2)}) copy-start(bf16[1920,240]{1,0:T(8,128)(2,1)} %all_gather.7) | copy-start | bytes 2764804
  122.3 3.5 %copy-start.3 = (bf16[2,2,120,120]{3,2,1,0:T(8,128)(2,1)S(1)}, bf16[2,2,120,120]{3,2,1,0:T(8,128)(2,1)}, u32[]{:S(2)}) copy-start(bf16[2,2,120,120]{3,2,1,0:T(8,128)(2,1)} %param.12) | copy-start | bytes 345604
  122.3 3.9 %copy-start.5 = (f32[2,120]{1,0:T(2,128)S(1)}, f32[2,120]{1,0:T(2,128)}, u32[]{:S(2)}) copy-start(f32[2,120]{1,0:T(2,128)} %param.14) | copy-start | bytes 2884
  122.3 4.9 %copy-start.7 = (s32[2,2]{1,0:T(2,128)S(1)}, s32[2,2]{1,0:T(2,128)}, u32[]{:S(2)}) copy-start(s32[2,2]{1,0:T(2,128)} %copy-done.6) | copy-start | bytes 52
  122.3 4.9 %copy-start.10 = (f32[32]{0:T(128)S(1)}, f32[32]{0:T(128)}, u32[]{:S(2)}) copy-start(f32[32]{0:T(128)} %param.15) | copy-start | bytes 388
  122.3 5.1 %copy-start.11 = (f32[2]{0:T(128)S(1)}, f32[2]{0:T(128)}, u32[]{:S(2)}) copy-start(f32[2]{0:T(128)} %constant.28.clone) | copy-start | bytes 28
  122.4 27.6 %all-to-all-start.1 = ((bf16[32,2,2,3600]{3,2,1,0:T(2,128)(2,1)}), bf16[32,2,2,3600]{3,2,1,0:T(2,128)(2,1)S(1)}, u32[]{:S(2)}, u32[]{:S(2)}) async-start(bf16[32,2,2,3600]{3,2,1,0:T(2,128)(2,1)} %bitcast.13), calls=%async_computation.1 | async-start | bytes 1900544 | tf_op jit(solution)/shard_map/all_to_all | solution.py:62
  125.9 24.9 %copy-start.4 = (f32[2,2,3600]{2,1,0:T(2,128)S(1)}, f32[2,2,3600]{2,1,0:T(2,128)}, u32[]{:S(2)}) copy-start(f32[2,2,3600]{2,1,0:T(2,128)} %param.13) | copy-start | bytes 172804

commit v2 on v1

--- a/solution.py
+++ b/solution.py
@@ -1,7 +1,13 @@
+import functools
+
 import jax
 import jax.numpy as jnp
 from jax import lax
+from jax.experimental import pallas as pl
+from jax.experimental.pallas import tpu as pltpu
 from jax.sharding import PartitionSpec as P
+
+LANE = 128
 
 
 def pair_weights(pair_lmo, neighbours, fock_off, first_pair):
@@ -21,7 +27,7 @@
     return (weights, own_table)
 
 
-def body(
+def plain_body(
     panels,
     amplitudes,
     drive,
@@ -74,6 +80,409 @@
     return drive + factor * amp_share + coupled_share
 
 
+def remote(src, dst, send_sem, recv_sem, pair, aux):
+    return pltpu.make_async_remote_copy(
+        src_ref=src,
+        dst_ref=dst,
+        send_sem=send_sem,
+        recv_sem=recv_sem,
+        device_id=(pair, aux),
+        device_id_type=pl.DeviceIdType.MESH,
+    )
+
+
+def kernel(
+    n_pair, n_aux, rank, x_ref, a_ref, w_ref, out_ref,
+    xb, ab, wb, left_rows, acc, parts, parts_in, sums, sums_in,
+    local_sem, x_send, x_recv, e_send, e_recv, f_send, f_recv, g_send, g_recv,
+    a_send, a_recv, b_send, b_recv, w_send, w_recv, y_send, y_recv, z_send, z_recv,
+):
+    me = lax.axis_index("pair")
+    aux = lax.axis_index("aux")
+    core = lax.rem(aux, 2)
+    chip = aux // 2
+    mate = aux + 1 - 2 * core
+    n_chip = n_aux // 2
+    block = 2 * rank
+    tiles = x_ref.shape[1] // LANE
+    base = (tiles // n_pair) * LANE
+    extra = tiles % n_pair
+    stride = n_pair // (2 * extra) if extra else 1
+    share = a_ref.shape[0] // n_aux
+    quarter = rank // n_aux
+    padded = parts.shape[2] // 2
+
+    barrier = pltpu.get_barrier_semaphore()
+
+    def greet(pair, other):
+        pl.semaphore_signal(
+            barrier, inc=1, device_id=(pair, other), device_id_type=pl.DeviceIdType.MESH
+        )
+
+    for t in range(1, n_pair):
+        peer = lax.rem(me + t, n_pair)
+        greet(peer, aux)
+        greet(peer, mate)
+    for t in range(1, n_aux):
+        greet(me, lax.rem(aux + t, n_aux))
+    pl.semaphore_wait(barrier, 2 * (n_pair - 1) + n_aux - 1)
+
+    def holder(which, level):
+        spot = 2 * level + which
+        shift = spot % 2 if not hasattr(spot, "dtype") else lax.rem(spot, 2)
+        return stride * spot + (shift if stride > 1 else 0)
+
+    lanes = pl.ds(pl.multiple_of(core * base, LANE), base)
+    mate_lanes = pl.ds(pl.multiple_of((1 - core) * base, LANE), base)
+    extra_lanes = pl.ds(2 * base, LANE)
+    my_share = pl.ds(pl.multiple_of(aux * share, 16), share)
+
+    def own_cols(peer):
+        return x_ref.at[:, pl.ds(pl.multiple_of(peer * base, LANE), base)]
+
+    def send_a(t):
+        peer = lax.rem(me + t, n_pair)
+        return remote(a_ref.at[my_share], ab.at[me, my_share], a_send.at[t], a_recv.at[me], peer, aux)
+
+    def send_w(t):
+        peer = lax.rem(me + t, n_pair)
+        return remote(w_ref, wb.at[me], w_send.at[t], w_recv.at[me], peer, aux)
+
+    def send_x(t):
+        peer = lax.rem(me + t, n_pair)
+        return remote(own_cols(peer), xb.at[me, :, lanes], x_send.at[t], x_recv.at[me], peer, aux)
+
+    def extra_cols(level):
+        return x_ref.at[:, pl.ds(base * n_pair + level * LANE, LANE)]
+
+    def send_e(level):
+        return remote(
+            extra_cols(level), xb.at[me, :, extra_lanes], e_send.at[level], e_recv.at[me],
+            holder(core, level), aux,
+        )
+
+    def send_f(j):
+        return remote(xb.at[j, :, lanes], xb.at[j, :, lanes], f_send.at[j], f_recv.at[j], me, mate)
+
+    def own_f():
+        return remote(own_cols(me), xb.at[me, :, lanes], f_send.at[me], f_recv.at[me], me, mate)
+
+    def send_g(j):
+        return remote(
+            xb.at[j, :, extra_lanes], xb.at[j, :, extra_lanes], g_send.at[j], g_recv.at[j], me, mate
+        )
+
+    def send_b(j, u):
+        rows = ab.at[j, my_share]
+        return remote(rows, rows, b_send.at[j, u], b_recv.at[aux, j], me, lax.rem(aux + u, n_aux))
+
+    mine_x = pltpu.make_async_copy(own_cols(me), xb.at[me, :, lanes], local_sem.at[0])
+    mine_a = pltpu.make_async_copy(a_ref, ab.at[me], local_sem.at[1])
+    mine_w = pltpu.make_async_copy(w_ref, wb.at[me], local_sem.at[2])
+    for t in range(1, n_pair):
+        send_a(t).start()
+    for t in range(1, n_pair):
+        send_w(t).start()
+    order = sorted(range(1, n_pair), key=lambda t: abs(n_pair // 2 - t))
+    for t in order:
+        send_x(t).start()
+    for level in range(extra):
+        @pl.when(holder(core, level) != me)
+        def _():
+            send_e(level).start()
+
+        @pl.when(holder(core, level) == me)
+        def _():
+            pltpu.make_async_copy(
+                extra_cols(level), xb.at[me, :, extra_lanes], local_sem.at[3]
+            ).start()
+    own_f().start()
+    mine_x.start()
+    mine_a.start()
+    mine_w.start()
+    acc[...] = jnp.zeros_like(acc)
+
+    def holds(which):
+        found = me < 0
+        for level in range(extra):
+            found = jnp.logical_or(found, holder(which, level) == me)
+        return found
+
+    self_holds = holds(core)
+    mate_holds = holds(1 - core)
+    if extra:
+        @pl.when(jnp.logical_not(jnp.logical_or(self_holds, mate_holds)))
+        def _():
+            xb[:, :, 2 * base :] = jnp.zeros((n_pair, block, LANE), xb.dtype)
+
+    for t in range(1, n_pair):
+        j = lax.rem(me + n_pair - t, n_pair)
+        remote(
+            a_ref.at[my_share], ab.at[j, my_share], a_send.at[t], a_recv.at[j], me, mate
+        ).wait_recv()
+        for u in range(1, n_aux):
+            send_b(j, u).start()
+    for t in order:
+        j = lax.rem(me + n_pair - t, n_pair)
+        remote(
+            own_cols(me), xb.at[j, :, lanes], x_send.at[t], x_recv.at[j], me, mate
+        ).wait_recv()
+        send_f(j).start()
+    mine_x.wait()
+    mine_a.wait()
+    mine_w.wait()
+    if extra:
+        @pl.when(self_holds)
+        def _():
+            pltpu.make_async_copy(
+                extra_cols(0), xb.at[me, :, extra_lanes], local_sem.at[3]
+            ).wait()
+            send_g(me).start()
+            for t in range(1, n_pair):
+                j = lax.rem(me + n_pair - t, n_pair)
+                remote(
+                    extra_cols(0), xb.at[j, :, extra_lanes], e_send.at[0], e_recv.at[j], me, mate
+                ).wait_recv()
+                send_g(j).start()
+
+        @pl.when(mate_holds)
+        def _():
+            for j in range(n_pair):
+                send_g(j).wait_recv()
+    for j in range(n_pair):
+        remote(
+            own_cols(me), xb.at[j, :, mate_lanes], f_send.at[j], f_recv.at[j], me, mate
+        ).wait_recv()
+    for t in range(1, n_pair):
+        j = lax.rem(me + n_pair - t, n_pair)
+        remote(w_ref, wb.at[j], w_send.at[t], w_recv.at[j], me, mate).wait_recv()
+        for u in range(1, n_aux):
+            other = lax.rem(aux + u, n_aux)
+            rows = ab.at[j, pl.ds(pl.multiple_of(other * share, 16), share)]
+            remote(rows, rows, b_send.at[j, u], b_recv.at[other, j], me, other).wait_recv()
+
+    for half in range(2):
+        @pl.when(core == half)
+        def _():
+            for i in range(n_pair):
+                left_rows[pl.ds(i * rank, rank), :] = xb[i, half * rank : (half + 1) * rank, :]
+
+    def couple(j, carry):
+        products = lax.dot_general(
+            left_rows[...], xb[j], (((1,), (1,)), ((), ())), preferred_element_type=jnp.float32
+        )
+        scaled = [
+            products[i * rank : (i + 1) * rank] * wb[i, core, pl.ds(j, 1), :]
+            for i in range(n_pair)
+        ]
+        mixed = jnp.concatenate(scaled, axis=0).astype(jnp.bfloat16)
+        turn = jnp.dot(mixed, ab[j, :block, :], preferred_element_type=jnp.float32)
+        for i in range(n_pair):
+            acc[i, :rank, :] += turn[i * rank : (i + 1) * rank]
+        return carry
+
+    lax.fori_loop(0, n_pair, couple, 0)
+
+    def send_y(i, u):
+        other = lax.rem(chip + u, n_chip)
+        return remote(
+            parts.at[other, i], parts_in.at[u, i], y_send.at[u, i], y_recv.at[u, i],
+            me, 2 * other + core,
+        )
+
+    def spread(t, carry):
+        i = lax.rem(me + 1 + t, n_pair)
+        for k in range(n_aux):
+            rows = acc[i, pl.ds(quarter * k, padded), :]
+            parts[k // 2, i, pl.ds((k % 2) * padded, padded), :] = rows.astype(parts.dtype)
+        for u in range(1, n_chip):
+            send_y(i, u).start()
+        return carry
+
+    lax.fori_loop(0, n_pair, spread, 0)
+
+    def send_z(i, to_core):
+        return remote(
+            sums.at[i, pl.ds(pl.multiple_of(to_core * padded, padded), padded)],
+            sums_in.at[me, core], z_send.at[i, to_core], z_recv.at[me, core],
+            i, 2 * chip + to_core,
+        )
+
+    def gather_sum(t, carry):
+        i = lax.rem(me + 1 + t, n_pair)
+        total = parts[chip, i].astype(jnp.float32)
+        for u in range(1, n_chip):
+            send_y(i, u).wait_recv()
+            total = total + parts_in[u, i].astype(jnp.float32)
+        sums[i] = total.astype(sums.dtype)
+
+        @pl.when(i != me)
+        def _():
+            send_z(i, core).start()
+
+        send_z(i, 1 - core).start()
+        return carry
+
+    lax.fori_loop(0, n_pair, gather_sum, 0)
+    sums_in[me, core] = sums[me, pl.ds(pl.multiple_of(core * padded, padded), padded), :]
+
+    def arrive(j, from_core):
+        remote(
+            sums.at[j, pl.ds(0, padded)], sums_in.at[j, from_core],
+            z_send.at[j, 0], z_recv.at[j, from_core], me, mate,
+        ).wait_recv()
+
+    for t in range(n_pair):
+        j = lax.rem(me + n_pair - t, n_pair)
+        if t:
+            arrive(j, core)
+        arrive(j, 1 - core)
+    for half in range(2):
+        total = sums_in[0, half].astype(jnp.float32)
+        for j in range(1, n_pair):
+            total = total + sums_in[j, half].astype(jnp.float32)
+        out_ref[half] = total
+
+    for t in range(1, n_pair):
+        send_a(t).wait_send()
+        send_w(t).wait_send()
+        send_x(t).wait_send()
+        j = lax.rem(me + n_pair - t, n_pair)
+        send_f(j).wait_send()
+        for u in range(1, n_aux):
+            send_b(j, u).wait_send()
+    own_f().wait_send()
+    for level in range(extra):
+        @pl.when(holder(core, level) != me)
+        def _():
+            send_e(level).wait_send()
+    if extra:
+        @pl.when(self_holds)
+        def _():
+            for j in range(n_pair):
+                send_g(j).wait_send()
+
+    def drain(i, carry):
+        for u in range(1, n_chip):
+            send_y(i, u).wait_send()
+
+        @pl.when(i != me)
+        def _():
+            send_z(i, core).wait_send()
+
+        send_z(i, 1 - core).wait_send()
+        return carry
+
+    lax.fori_loop(0, n_pair, drain, 0)
+
+
+def fused_coupling(x_own, a_own, w_own, n_pair, n_aux, rank):
+    block = 2 * rank
+    tiles = x_own.shape[1] // LANE
+    depth = 2 * (tiles // n_pair) * LANE + (LANE if tiles % n_pair else 0)
+    n_chip = n_aux // 2
+    extra = max(tiles % n_pair, 1)
+    padded = -(-(rank // n_aux) // 16) * 16
+    tall = -(-(rank - rank // n_aux + padded) // 8) * 8
+    dma = pltpu.SemaphoreType.DMA
+    bf16 = jnp.bfloat16
+    return pl.pallas_call(
+        functools.partial(kernel, n_pair, n_aux, rank),
+        out_shape=jax.ShapeDtypeStruct((2, padded, block), jnp.float32),
+        in_specs=[pl.BlockSpec(memory_space=pltpu.VMEM)] * 3,
+        out_specs=pl.BlockSpec(memory_space=pltpu.VMEM),
+        scratch_shapes=[
+            pltpu.VMEM((n_pair, block, depth), bf16),
+            pltpu.VMEM((n_pair,) + a_own.shape, bf16),
+            pltpu.VMEM((n_pair,) + w_own.shape, jnp.float32),
+            pltpu.VMEM((n_pair * rank, depth), bf16),
+            pltpu.VMEM((n_pair, tall, block), jnp.float32),
+            pltpu.VMEM((n_chip, n_pair, 2 * padded, block), bf16),
+            pltpu.VMEM((n_chip, n_pair, 2 * padded, block), bf16),
+            pltpu.VMEM((n_pair, 2 * padded, block), bf16),
+            pltpu.VMEM((n_pair, 2, padded, block), bf16),
+            dma((4,)),
+            dma((n_pair,)), dma((n_pair,)),
+            dma((extra,)), dma((n_pair,)),
+            dma((n_pair,)), dma((n_pair,)),
+            dma((n_pair,)), dma((n_pair,)),
+            dma((n_pair,)), dma((n_pair,)),
+            dma((n_pair, n_aux)), dma((n_aux, n_pair)),
+            dma((n_pair,)), dma((n_pair,)),
+            dma((n_chip, n_pair)), dma((n_chip, n_pair)),
+            dma((n_pair, 2)), dma((n_pair, 2)),
+        ],
+        compiler_params=pltpu.CompilerParams(collective_id=0, has_side_effects=True),
+    )(x_own, a_own, w_own)
+
+
+def fits(panels, n_pair, n_aux):
+    local_pairs, rank, width = panels.shape
+    tiles = width // LANE
+    extra = tiles % n_pair
+    return (
+        local_pairs == 2
+        and width % LANE == 0
+        and rank % 8 == 0
+        and rank % n_aux == 0
+        and n_aux % 2 == 0
+        and n_pair > 1
+        and tiles >= n_pair
+        and (extra == 0 or n_pair % (2 * extra) == 0)
+    )
+
+
+def body(*operands):
+    if fits(operands[0], lax.axis_size("pair"), lax.axis_size("aux")):
+        return kernel_body(*operands)
+    return plain_body(*operands)
+
+
+def kernel_body(
+    panels,
+    amplitudes,
+    drive,
+    pno_energy,
+    occ_energy,
+    frequency,
+    pair_lmo,
+    neighbours,
+    pno_ranks,
+    fock_off,
+):
+    local_pairs, rank_dim, aux_width = panels.shape
+    n_pair = lax.axis_size("pair")
+    n_aux = lax.axis_size("aux")
+    first_pair = lax.axis_index("pair") * local_pairs
+    rows_index = jnp.arange(rank_dim, dtype=jnp.int32)
+    keep_rows = rows_index[None, :] < pno_ranks[:, None]
+    weights, own_table = pair_weights(pair_lmo, neighbours, fock_off, first_pair)
+    w_own = jnp.repeat(
+        weights.astype(jnp.float32).reshape(local_pairs, n_pair, local_pairs), rank_dim, axis=2
+    )
+    amps = jnp.where(keep_rows[:, :, None, None], jnp.transpose(amplitudes, (0, 2, 1, 3)), 0)
+    amps = amps.reshape(2 * rank_dim, 2 * rank_dim)
+    tall = -(-2 * rank_dim // (16 * n_aux)) * 16 * n_aux
+    amps = jnp.pad(amps, ((0, tall - 2 * rank_dim), (0, 0)))
+    sums = fused_coupling(
+        panels.reshape(2 * rank_dim, aux_width), amps, w_own, n_pair, n_aux, rank_dim
+    )
+    share_width = drive.shape[2]
+    quarter = rank_dim // n_aux
+    row_start = lax.axis_index("aux") * quarter
+    keep_share = lax.dynamic_slice_in_dim(keep_rows, row_start, quarter, 1)
+    coupled = sums[:, :quarter].reshape(local_pairs, quarter, 2, rank_dim)
+    coupled = jnp.where(keep_share[:, :, None, None], coupled, 0.0).transpose(0, 2, 1, 3)
+    occ_pair = jnp.sum(own_table * occ_energy[None, None, :], axis=(1, 2))
+    energy_rows = lax.dynamic_slice_in_dim(pno_energy, row_start, quarter, 1)
+    shift = energy_rows[:, :, None] + pno_energy[:, None, :] - occ_pair[:, None, None]
+    signs = jnp.array([1.0, -1.0], jnp.float32)
+    factor = shift[:, None] - signs[None, :, None, None] * frequency[0]
+    amp_share = lax.dynamic_slice_in_dim(amplitudes, row_start, quarter, 2).astype(jnp.float32)
+    rest = (factor * amp_share + coupled).reshape(local_pairs, 2, share_width)
+    return drive + rest
+
+
 def solution(mesh):
     placed = (
         P("pair", None, "aux"),

time: 152 us -> 70.8 us (0.47)
  blocking collectives: 70.4 us -> 0 us
  Pallas kernels: 0 us -> 61.5 us
  local copies, waits for them, and re-layouts: 30.6 us -> 4.76 us
  waiting for transfers between devices: 22.5 us -> 0 us
  matrix products: 11.4 us -> 0.48 us
  starting transfers between devices: 10.9 us -> 0 us
  other arithmetic: 4.79 us -> 2.89 us
    all_gather x2 -> x0, blocking collectives: 70.4 us -> none  [the longest x1 37.1 us: body(): lax.all_gather(amps.reshape(local_pairs * rank_dim, 2 * rank_dim), 'pair'...]
    pallas_call x0 -> x1, Pallas kernels: none -> 61.5 us  [fused_coupling(): pl.pallas_call(functools.partial(kernel, n_pair, n_aux, rank), out_shape=...]
    all_to_all x2 -> x0, waiting for transfers between devices: 22.5 us -> none  [the longest x1 22.5 us: body(): coupled = lax.all_to_all(coupled, ('pair', 'aux'), 0, 0, tiled=True)]
    reshape x6 -> x4, local copies, waits for them, and re-layouts: 19.3 us -> 1.89 us  [the longest x1 0.94 us: kernel_body(): coupled = sums[:, :quarter].reshape(local_pairs, quarter, 2, rank_dim)]
    all_to_all x2 -> x0, starting transfers between devices: 10.9 us -> none  [the longest x1 7.41 us: body(): lax.all_to_all(masked.reshape(local_pairs * rank_dim, aux_width), 'pair',...]
    dot_general x2 -> x0, matrix products: 10.9 us -> none  [the longest x1 5.48 us: body(): jnp.einsum('iq,jq->ij', slices, slices, preferred_element_type=jnp.float32)]
    convert_element_type x1, local copies, waits for them, and re-layouts: 4.73 us -> 0.08 us  [kernel_body(): weights.astype(jnp.float32).reshape(local_pairs, n_pair, local_pairs)]
    all_to_all x2 -> x0, local copies, waits for them, and re-layouts: 2.22 us -> none  [body(): lax.all_to_all(masked.reshape(local_pairs * rank_dim, aux_width), 'pair',...]
  transfers between devices with their start and end apart: 2 -> 0, of which waited for: 1 -> 0; matrix products, arithmetic and copies ran while one was open for 2% -> 0% of each run, Pallas kernels for 0% -> 0%
where the time goes in v2:
time: 70.8 us; the launch traced here: 70.4 us
  Pallas kernels  61.5 us (87%)
  local copies, waits for them, and re-layouts  4.76 us (7%)
  other arithmetic  2.89 us (4%)
  between operations  0.8 us (1%)
    pallas_call x1, Pallas kernels, fused_coupling(): pl.pallas_call(functools.partial(kernel, n_pair, n_aux, rank), out_shape=...  61.5 us

profile of v2, /device:TPU:0, one launch (start us, length us, event | category | flops | bytes accessed | tf_op | source)
XLA Modules:
  0.0 70.4 jit_solution(15917696121689463816)
XLA Ops:
  0.0 0.0 copy-start
  0.0 0.7 %iota_compare_fusion = pred[2,120]{0,1:T(8,128)(4,1)S(1)} fusion(s32[2]{0:T(128)} %param.19), kind=kLoop, calls=%fused_computation.5 | loop fusion | flops 240 | bytes 248 | tf_op jit(solution)/shard_map/lt | solution.py:458
  0.7 0.1 copy.24
  0.8 1.0 %select_bitcast_fusion = bf16[2,120,2,120]{3,1,2,0:T(8,128)(2,1)S(1)} fusion(bf16[2,2,120,120]{3,2,1,0:T(8,128)(2,1)} %param.12, pred[2,120]{1,0:T(4,128)(4,1)S(1)} %copy.24), kind=kLoop, calls=%fused_computation.2 | loop fusion | flops 57600 | bytes 230640 | tf_op jit(solution)/shard_map/jit(_where)/select_n | solution.py:463
  1.8 0.1 copy.25
  1.9 0.0 copy-start.5
  1.9 0.0 copy-start.2
  2.0 0.1 reshape.55
  2.1 0.0 copy-start.6
  2.1 0.7 pad.4.a_ref
  2.7 0.7 %constant_dynamic-slice_fusion.2 = s32[2,2]{0,1:T(2,128)S(1)} fusion(s32[16,2]{0,1:T(2,128)} %param.17, s32[]{:T(128)S(6)} %select_n.20), kind=kLoop, calls=%fused_computation.21 | loop fusion | bytes 36 | tf_op jit(solution)/shard_map/dynamic_slice | solution.py:18
  3.5 0.1 copy.22
  3.6 0.0 copy-done
  3.6 0.2 fusion.1
  3.8 0.0 copy-done.3
  3.8 0.0 copy-start.1
  3.8 0.3 fusion
  4.1 0.1 select_reduce_fusion
  4.2 0.1 reshape.59
  4.3 0.1 broadcast_in_dim.29
  4.3 0.7 reshape.56.w_ref
  5.1 61.5 %shard_map.109 = f32[2,32,240]{2,1,0:T(8,128)} custom-call(bf16[240,2304]{1,0:T(8,128)(2,1)} %bitcast.19, bf16[256,240]{1,0:T(8,128)(2,1)} %pad.4.a_ref, f32[2,8,240]{2,1,0:T(8,128)} %reshape.56.w_ref), custom_call_target="tpu_custom_call" | custom-call | tf_op jit(solution)/shard_map/pallas_call | solution.py:389
  66.6 0.9 %reshape.63 = f32[2,30,2,120]{3,2,1,0:T(2,128)S(1)} reshape(f32[2,30,240]{2,1,0:T(8,128)} %bitcast.20) | data formatting | bytes 115200 | tf_op jit(solution)/shard_map/reshape | solution.py:474
  67.5 0.8 %constant_dynamic-slice_fusion.1 = bf16[2,2,30,120]{3,2,1,0:T(8,128)(2,1)S(1)} fusion(bf16[2,2,120,120]{3,2,1,0:T(8,128)(2,1)} %param.12, s32[]{:T(128)S(6)} %select_n.19), kind=kLoop, calls=%fused_computation.20 | loop fusion | bytes 57604 | tf_op jit(solution)/shard_map/dynamic_slice | solution.py:481
  68.4 0.2 select_reduce_fusion.1
  68.5 0.1 constant_dynamic-slice_fusion.3
  68.6 0.1 copy.21
  68.7 0.1 add_subtract_fusion
  69.5 0.0 copy-done.6
  69.5 0.1 bitcast_add_fusion
  69.6 0.1 reshape.58
  69.8 0.7 add.39
  (9 shorter events, 0.0 us)
Async XLA Ops:
  0.0 3.6 %copy-start = (f32[32,32]{1,0:T(8,128)S(1)}, f32[32,32]{1,0:T(8,128)}, u32[]{:S(2)}) copy-start(f32[32,32]{1,0:T(8,128)} %param.20) | copy-start | bytes 12292
  0.0 3.8 %copy-start.3 = (s32[16,2]{0,1:T(2,128)S(1)}, s32[16,2]{0,1:T(2,128)}, u32[]{:S(2)}) copy-start(s32[16,2]{0,1:T(2,128)} %param.17) | copy-start | bytes 388
  0.0 3.8 %copy-start.4 = (s32[2,8]{1,0:T(2,128)S(1)}, s32[2,8]{1,0:T(2,128)}, u32[]{:S(2)}) copy-start(s32[2,8]{1,0:T(2,128)} %param.18) | copy-start | bytes 196
  1.9 66.4 %copy-start.5 = (f32[32]{0:T(128)S(1)}, f32[32]{0:T(128)}, u32[]{:S(2)}) copy-start(f32[32]{0:T(128)} %param.15) | copy-start | bytes 388
  1.9 66.6 %copy-start.2 = (f32[2,120]{1,0:T(2,128)S(1)}, f32[2,120]{1,0:T(2,128)}, u32[]{:S(2)}) copy-start(f32[2,120]{1,0:T(2,128)} %param.14) | copy-start | bytes 2884
  2.1 67.4 %copy-start.6 = (f32[2]{0:T(128)S(1)}, f32[2]{0:T(128)}, u32[]{:S(2)}) copy-start(f32[2]{0:T(128)} %constant.27.clone) | copy-start | bytes 28
  3.8 66.0 %copy-start.1 = (f32[2,2,3600]{2,1,0:T(2,128)S(1)}, f32[2,2,3600]{2,1,0:T(2,128)}, u32[]{:S(2)}) copy-start(f32[2,2,3600]{2,1,0:T(2,128)} %param.13) | copy-start | bytes 172804

commit v3 on v2

--- a/solution.py
+++ b/solution.py
@@ -93,7 +93,7 @@
 
 def kernel(
     n_pair, n_aux, rank, x_ref, a_ref, w_ref, out_ref,
-    xb, ab, wb, left_rows, acc, parts, parts_in, sums, sums_in,
+    xb, ab, wb, wt, left_rows, acc, parts, parts_in, sums, sums_in,
     local_sem, x_send, x_recv, e_send, e_recv, f_send, f_recv, g_send, g_recv,
     a_send, a_recv, b_send, b_recv, w_send, w_recv, y_send, y_recv, z_send, z_recv,
 ):
@@ -140,17 +140,48 @@
     def own_cols(peer):
         return x_ref.at[:, pl.ds(pl.multiple_of(peer * base, LANE), base)]
 
+    half = n_pair // 2
+    near = (me // half) * half
+    far = half - near
+    across = lax.rem(me + half, n_pair)
+
+    def near_peer(t):
+        return near + lax.rem(me - near + t, half)
+
+    def far_peer(t):
+        return far + lax.rem(me - near + t, half)
+
     def send_a(t):
-        peer = lax.rem(me + t, n_pair)
+        peer = near_peer(t) if t else across
         return remote(a_ref.at[my_share], ab.at[me, my_share], a_send.at[t], a_recv.at[me], peer, aux)
+
+    def pass_a(t):
+        rows = ab.at[across, my_share]
+        return remote(rows, rows, a_send.at[half + t], a_recv.at[across], near_peer(t), aux)
+
+    def wait_a(j):
+        remote(
+            a_ref.at[my_share], ab.at[j, my_share], a_send.at[0], a_recv.at[j], me, mate
+        ).wait_recv()
 
     def send_w(t):
         peer = lax.rem(me + t, n_pair)
         return remote(w_ref, wb.at[me], w_send.at[t], w_recv.at[me], peer, aux)
 
-    def send_x(t):
-        peer = lax.rem(me + t, n_pair)
-        return remote(own_cols(peer), xb.at[me, :, lanes], x_send.at[t], x_recv.at[me], peer, aux)
+    def send_x(peer):
+        return remote(
+            own_cols(peer), xb.at[me, :, lanes], x_send.at[peer], x_recv.at[me], peer, aux
+        )
+
+    def wait_x(j):
+        remote(
+            own_cols(me), xb.at[j, :, lanes], x_send.at[j], x_recv.at[j], me, mate
+        ).wait_recv()
+
+    def wait_f(j):
+        remote(
+            own_cols(me), xb.at[j, :, mate_lanes], f_send.at[j], f_recv.at[j], me, mate
+        ).wait_recv()
 
     def extra_cols(level):
         return x_ref.at[:, pl.ds(base * n_pair + level * LANE, LANE)]
@@ -179,13 +210,10 @@
     mine_x = pltpu.make_async_copy(own_cols(me), xb.at[me, :, lanes], local_sem.at[0])
     mine_a = pltpu.make_async_copy(a_ref, ab.at[me], local_sem.at[1])
     mine_w = pltpu.make_async_copy(w_ref, wb.at[me], local_sem.at[2])
-    for t in range(1, n_pair):
+    for t in range(half):
         send_a(t).start()
     for t in range(1, n_pair):
         send_w(t).start()
-    order = sorted(range(1, n_pair), key=lambda t: abs(n_pair // 2 - t))
-    for t in order:
-        send_x(t).start()
     for level in range(extra):
         @pl.when(holder(core, level) != me)
         def _():
@@ -196,6 +224,8 @@
             pltpu.make_async_copy(
                 extra_cols(level), xb.at[me, :, extra_lanes], local_sem.at[3]
             ).start()
+    for t in range(half):
+        send_x(far_peer(t)).start()
     own_f().start()
     mine_x.start()
     mine_a.start()
@@ -215,19 +245,18 @@
         def _():
             xb[:, :, 2 * base :] = jnp.zeros((n_pair, block, LANE), xb.dtype)
 
-    for t in range(1, n_pair):
-        j = lax.rem(me + n_pair - t, n_pair)
-        remote(
-            a_ref.at[my_share], ab.at[j, my_share], a_send.at[t], a_recv.at[j], me, mate
-        ).wait_recv()
-        for u in range(1, n_aux):
-            send_b(j, u).start()
-    for t in order:
-        j = lax.rem(me + n_pair - t, n_pair)
-        remote(
-            own_cols(me), xb.at[j, :, lanes], x_send.at[t], x_recv.at[j], me, mate
-        ).wait_recv()
-        send_f(j).start()
+    wait_a(across)
+    for t in range(1, half):
+        pass_a(t).start()
+    for t in range(1, half):
+        send_x(near_peer(t)).start()
+    for t in range(half):
+        arrived = [far_peer(t)] if t == 0 else [near_peer(half - t), far_peer(half - t)]
+        for j in arrived:
+            if t:
+                wait_a(j)
+            for u in range(1, n_aux):
+                send_b(j, u).start()
     mine_x.wait()
     mine_a.wait()
     mine_w.wait()
@@ -249,10 +278,10 @@
         def _():
             for j in range(n_pair):
                 send_g(j).wait_recv()
-    for j in range(n_pair):
-        remote(
-            own_cols(me), xb.at[j, :, mate_lanes], f_send.at[j], f_recv.at[j], me, mate
-        ).wait_recv()
+    for t in range(1, half):
+        j = near_peer(half - t)
+        wait_x(j)
+        send_f(j).start()
     for t in range(1, n_pair):
         j = lax.rem(me + n_pair - t, n_pair)
         remote(w_ref, wb.at[j], w_send.at[t], w_recv.at[j], me, mate).wait_recv()
@@ -260,28 +289,59 @@
             other = lax.rem(aux + u, n_aux)
             rows = ab.at[j, pl.ds(pl.multiple_of(other * share, 16), share)]
             remote(rows, rows, b_send.at[j, u], b_recv.at[other, j], me, other).wait_recv()
-
-    for half in range(2):
-        @pl.when(core == half)
-        def _():
-            for i in range(n_pair):
-                left_rows[pl.ds(i * rank, rank), :] = xb[i, half * rank : (half + 1) * rank, :]
-
-    def couple(j, carry):
+    table = wb[...]
+    table = jnp.where(core == 0, table[:, 0], table[:, 1]).astype(jnp.bfloat16)
+    pair_row = lax.broadcasted_iota(jnp.int32, (LANE, block), 0)
+    column = lax.broadcasted_iota(jnp.int32, (LANE, block), 1)
+    for j in range(n_pair):
+        pick = pair_row == jnp.where(column < rank, 2 * j, 2 * j + 1)
+        pick = jnp.where(pick, 1.0, 0.0).astype(jnp.bfloat16)
+        wt[j] = jnp.dot(table, pick, preferred_element_type=jnp.float32)
+
+    def collect_rows(start):
+        for side in range(2):
+            @pl.when(core == side)
+            def _():
+                for i in range(half):
+                    left_rows[start + i] = xb[start + i, side * rank : (side + 1) * rank, :]
+
+    def couple(start, j):
+        rows = jnp.concatenate([left_rows[start + i] for i in range(half)], axis=0)
         products = lax.dot_general(
-            left_rows[...], xb[j], (((1,), (1,)), ((), ())), preferred_element_type=jnp.float32
+            rows, xb[j], (((1,), (1,)), ((), ())), preferred_element_type=jnp.float32
         )
         scaled = [
-            products[i * rank : (i + 1) * rank] * wb[i, core, pl.ds(j, 1), :]
-            for i in range(n_pair)
+            products[i * rank : (i + 1) * rank] * wt[j, pl.ds(start + i, 1), :]
+            for i in range(half)
         ]
         mixed = jnp.concatenate(scaled, axis=0).astype(jnp.bfloat16)
         turn = jnp.dot(mixed, ab[j, :block, :], preferred_element_type=jnp.float32)
-        for i in range(n_pair):
-            acc[i, :rank, :] += turn[i * rank : (i + 1) * rank]
+        for i in range(half):
+            acc[start + i, :rank, :] += turn[i * rank : (i + 1) * rank]
+
+    for t in range(half):
+        wait_f(near_peer(t))
+    collect_rows(near)
+
+    def near_near(t, carry):
+        couple(near, near + t)
         return carry
 
-    lax.fori_loop(0, n_pair, couple, 0)
+    lax.fori_loop(0, half, near_near, 0)
+
+    def near_far(t, carry):
+        j = far_peer(lax.rem(half - t, half))
+        wait_x(j)
+        send_f(j).start()
+        wait_f(j)
+        couple(near, j)
+        return carry
+
+    lax.fori_loop(0, half, near_far, 0)
+
+    def far_all(j, carry):
+        couple(far, j)
+        return carry
 
     def send_y(i, u):
         other = lax.rem(chip + u, n_chip)
@@ -290,8 +350,12 @@
             me, 2 * other + core,
         )
 
+    def turn_pair(t):
+        side = jnp.where(t < half, near, far)
+        return side + lax.rem(me - near + 1 + t, half)
+
     def spread(t, carry):
-        i = lax.rem(me + 1 + t, n_pair)
+        i = turn_pair(t)
         for k in range(n_aux):
             rows = acc[i, pl.ds(quarter * k, padded), :]
             parts[k // 2, i, pl.ds((k % 2) * padded, padded), :] = rows.astype(parts.dtype)
@@ -299,7 +363,10 @@
             send_y(i, u).start()
         return carry
 
-    lax.fori_loop(0, n_pair, spread, 0)
+    lax.fori_loop(0, half, spread, 0)
+    collect_rows(far)
+    lax.fori_loop(0, n_pair, far_all, 0)
+    lax.fori_loop(half, n_pair, spread, 0)
 
     def send_z(i, to_core):
         return remote(
@@ -309,7 +376,7 @@
         )
 
     def gather_sum(t, carry):
-        i = lax.rem(me + 1 + t, n_pair)
+        i = turn_pair(t)
         total = parts[chip, i].astype(jnp.float32)
         for u in range(1, n_chip):
             send_y(i, u).wait_recv()
@@ -337,16 +404,20 @@
         if t:
             arrive(j, core)
         arrive(j, 1 - core)
-    for half in range(2):
-        total = sums_in[0, half].astype(jnp.float32)
+    for side in range(2):
+        total = sums_in[0, side].astype(jnp.float32)
         for j in range(1, n_pair):
-            total = total + sums_in[j, half].astype(jnp.float32)
-        out_ref[half] = total
-
+            total = total + sums_in[j, side].astype(jnp.float32)
+        out_ref[side] = total
+
+    for t in range(half):
+        send_a(t).wait_send()
+        send_x(far_peer(t)).wait_send()
+        if t:
+            pass_a(t).wait_send()
+            send_x(near_peer(t)).wait_send()
     for t in range(1, n_pair):
-        send_a(t).wait_send()
         send_w(t).wait_send()
-        send_x(t).wait_send()
         j = lax.rem(me + n_pair - t, n_pair)
         send_f(j).wait_send()
         for u in range(1, n_aux):
@@ -395,7 +466,8 @@
             pltpu.VMEM((n_pair, block, depth), bf16),
             pltpu.VMEM((n_pair,) + a_own.shape, bf16),
             pltpu.VMEM((n_pair,) + w_own.shape, jnp.float32),
-            pltpu.VMEM((n_pair * rank, depth), bf16),
+            pltpu.VMEM((n_pair, n_pair, block), jnp.float32),
+            pltpu.VMEM((n_pair, rank, depth), bf16),
             pltpu.VMEM((n_pair, tall, block), jnp.float32),
             pltpu.VMEM((n_chip, n_pair, 2 * padded, block), bf16),
             pltpu.VMEM((n_chip, n_pair, 2 * padded, block), bf16),
@@ -426,7 +498,8 @@
         and rank % 8 == 0
         and rank % n_aux == 0
         and n_aux % 2 == 0
-        and n_pair > 1
+        and n_pair % 2 == 0
+        and 2 * n_pair <= LANE
         and tiles >= n_pair
         and (extra == 0 or n_pair % (2 * extra) == 0)
     )
@@ -457,9 +530,7 @@
     rows_index = jnp.arange(rank_dim, dtype=jnp.int32)
     keep_rows = rows_index[None, :] < pno_ranks[:, None]
     weights, own_table = pair_weights(pair_lmo, neighbours, fock_off, first_pair)
-    w_own = jnp.repeat(
-        weights.astype(jnp.float32).reshape(local_pairs, n_pair, local_pairs), rank_dim, axis=2
-    )
+    w_own = jnp.pad(weights.astype(jnp.float32), ((0, 0), (0, LANE - weights.shape[1])))
     amps = jnp.where(keep_rows[:, :, None, None], jnp.transpose(amplitudes, (0, 2, 1, 3)), 0)
     amps = amps.reshape(2 * rank_dim, 2 * rank_dim)
     tall = -(-2 * rank_dim // (16 * n_aux)) * 16 * n_aux

time: 70.8 us -> 67.6 us (0.955)
  Pallas kernels: 61.5 us -> 58.6 us
  local copies, waits for them, and re-layouts: 4.76 us -> 3.9 us
    pallas_call x1, Pallas kernels: 61.5 us -> 58.6 us  [fused_coupling(): pl.pallas_call(functools.partial(kernel, n_pair, n_aux, rank), out_shape=...]
where the time goes in v3:
time: 67.6 us; the launch traced here: 67.3 us
  Pallas kernels  58.6 us (87%)
  local copies, waits for them, and re-layouts  3.9 us (6%)
  other arithmetic  3.46 us (5%)
  between operations  0.79 us (1%)
    pallas_call x1, Pallas kernels, fused_coupling(): pl.pallas_call(functools.partial(kernel, n_pair, n_aux, rank), out_shape=...  58.6 us

profile of v3, /device:TPU:0, one launch (start us, length us, event | category | flops | bytes accessed | tf_op | source)
XLA Modules:
  0.0 67.3 jit_solution(8576467649835006478)
XLA Ops:
  0.0 0.0 copy-start
  0.0 0.7 %iota_compare_fusion = pred[2,120]{0,1:T(8,128)(4,1)S(1)} fusion(s32[2]{0:T(128)} %param.19), kind=kLoop, calls=%fused_computation.5 | loop fusion | flops 240 | bytes 248 | tf_op jit(solution)/shard_map/lt | solution.py:531
  0.7 0.1 copy.24
  0.8 1.0 %select_bitcast_fusion = bf16[2,120,2,120]{3,1,2,0:T(8,128)(2,1)S(1)} fusion(bf16[2,2,120,120]{3,2,1,0:T(8,128)(2,1)} %param.12, pred[2,120]{1,0:T(4,128)(4,1)S(1)} %copy.24), kind=kLoop, calls=%fused_computation.2 | loop fusion | flops 57600 | bytes 230640 | tf_op jit(solution)/shard_map/jit(_where)/select_n | solution.py:534
  1.8 0.1 copy.25
  1.9 0.0 copy-start.5
  1.9 0.0 copy-start.2
  2.0 0.0 copy-start.6
  2.0 0.1 reshape.47
  2.1 0.7 pad.10.a_ref
  2.7 0.7 %constant_dynamic-slice_fusion.2 = s32[2,2]{0,1:T(2,128)S(1)} fusion(s32[16,2]{0,1:T(2,128)} %param.17, s32[]{:T(128)S(6)} %select_n.20), kind=kLoop, calls=%fused_computation.21 | loop fusion | bytes 36 | tf_op jit(solution)/shard_map/dynamic_slice | solution.py:18
  3.5 0.1 copy.22
  3.6 0.0 copy-done
  3.6 0.2 fusion.1
  3.8 0.0 copy-done.3
  3.8 0.0 copy-done.4
  3.8 0.3 fusion
  4.1 0.1 select_reduce_fusion
  4.2 0.6 pad_convert_fusion.w_ref
  4.8 58.6 %shard_map.109 = f32[2,32,240]{2,1,0:T(8,128)} custom-call(bf16[240,2304]{1,0:T(8,128)(2,1)} %bitcast.19, bf16[256,240]{1,0:T(8,128)(2,1)} %pad.10.a_ref, f32[2,128]{1,0:T(2,128)} %pad_convert_fusion.w_ref), custom_call_target="tpu_custom_call" | custom-call | tf_op jit(solution)/shard_map/pallas_call | solution.py:460
  63.4 0.9 %reshape.53 = f32[2,30,2,120]{3,2,1,0:T(2,128)S(1)} reshape(f32[2,30,240]{2,1,0:T(8,128)} %bitcast.20) | data formatting | bytes 115200 | tf_op jit(solution)/shard_map/reshape | solution.py:545
  64.4 0.8 %constant_dynamic-slice_fusion.1 = bf16[2,2,30,120]{3,2,1,0:T(8,128)(2,1)S(1)} fusion(bf16[2,2,120,120]{3,2,1,0:T(8,128)(2,1)} %param.12, s32[]{:T(128)S(6)} %select_n.19), kind=kLoop, calls=%fused_computation.20 | loop fusion | bytes 57604 | tf_op jit(solution)/shard_map/dynamic_slice | solution.py:552
  65.2 0.0 copy-done.5
  65.2 0.2 select_reduce_fusion.1
  65.4 0.0 copy-done.2
  65.4 0.1 constant_dynamic-slice_fusion.3
  65.4 0.1 copy.21
  65.5 0.1 add_subtract_fusion
  66.3 0.1 bitcast_add_fusion
  66.5 0.1 reshape.49
  66.6 0.0 copy-done.1
  66.6 0.7 add.41
  (7 shorter events, 0.0 us)
Async XLA Ops:
  0.0 3.6 %copy-start = (f32[32,32]{1,0:T(8,128)S(1)}, f32[32,32]{1,0:T(8,128)}, u32[]{:S(2)}) copy-start(f32[32,32]{1,0:T(8,128)} %param.20) | copy-start | bytes 12292
  0.0 3.8 %copy-start.3 = (s32[16,2]{0,1:T(2,128)S(1)}, s32[16,2]{0,1:T(2,128)}, u32[]{:S(2)}) copy-start(s32[16,2]{0,1:T(2,128)} %param.17) | copy-start | bytes 388
  0.0 3.8 %copy-start.4 = (s32[2,8]{1,0:T(2,128)S(1)}, s32[2,8]{1,0:T(2,128)}, u32[]{:S(2)}) copy-start(s32[2,8]{1,0:T(2,128)} %param.18) | copy-start | bytes 196
  1.9 63.2 %copy-start.5 = (f32[32]{0:T(128)S(1)}, f32[32]{0:T(128)}, u32[]{:S(2)}) copy-start(f32[32]{0:T(128)} %param.15) | copy-start | bytes 388
  1.9 63.4 %copy-start.2 = (f32[2,120]{1,0:T(2,128)S(1)}, f32[2,120]{1,0:T(2,128)}, u32[]{:S(2)}) copy-start(f32[2,120]{1,0:T(2,128)} %param.14) | copy-start | bytes 2884
  2.0 64.3 %copy-start.6 = (f32[2]{0:T(128)S(1)}, f32[2]{0:T(128)}, u32[]{:S(2)}) copy-start(f32[2]{0:T(128)} %constant.29.clone) | copy-start | bytes 28
  3.6 63.0 %copy-start.1 = (f32[2,2,3600]{2,1,0:T(2,128)S(1)}, f32[2,2,3600]{2,1,0:T(2,128)}, u32[]{:S(2)}) copy-start(f32[2,2,3600]{2,1,0:T(2,128)} %param.13) | copy-start | bytes 172804
